TPU v7x, 32 devices: a whole 2x2x4 slice. The times are simulated.
32 devices in a mesh: dp: 8 (over y, x, core), mp: 4 (over z).
Axes of the slice: x: 2, y: 2, z: 4, core: 2. Of those that a mesh axis runs over, the one named last changes fastest.
Arguments:
- acts: bfloat16 [4096, 3072], P('dp'), may hold values from -16 to 16
- grads_out: bfloat16 [4096, 8192], P('dp', 'mp'), may hold values from -0.125 to 0.125
- old_a: float32 [8, 3, 128, 1024], P('dp'), may hold values from -0.09375 to 0.09375
- old_g: float32 [4, 8, 2, 128, 1024], P('mp', 'dp'), may hold values from -0.09375 to 0.09375
- a_inverse: bfloat16 [3072, 1024], P('dp'), may hold values from -0.1875 to 0.1875
- g_inverse: bfloat16 [8192, 1024], P('mp'), may hold values from -0.1875 to 0.1875
- owner_map: int32 [5, 8], replicated, may hold values from 0 to 7, each once within a row
Outputs:
- a_factor: float32 [8, 3, 128, 1024], P('dp')
- g_factor: float32 [4, 8, 2, 128, 1024], P('mp', 'dp')
- preconditioned: bfloat16 [3072, 4, 2048], P(None, 'mp', 'dp')
Inputs may be any that keep to these rules, and one draw needn't show every extreme that they name: `owner_map`: each row is a permutation: row k tells, for each of the 8 row strips of factor block k, which dp index holds it. Rows 0 to 2 are the activation blocks, the others the output-gradient blocks of every mp index.
All inputs are finite; a program needn't handle non-finite values.
Results may differ from a plain program's by a relative error of at most 0.02.
Values may be sent and summed in bfloat16 or wider, within the bound.
A program may use at most 128 MiB of HBM per device.

v0:
```python
import jax
import jax.numpy as jnp
from jax import lax
from jax.sharding import PartitionSpec as P

D_WIN = 3072
BLOCK = 1024
FF_DEV = 2048
TOK_DEV = 512
NA = 3
NG = 2
decay_rate = 0.75


def to_owner(stacked, where_from):
    return jnp.take_along_axis(stacked, where_from[:, :, None, None], axis=1)


def per_device(acts, grads_out, old_a, old_g, a_inverse, g_inverse, owner_map):
    dp_count = lax.axis_size("dp")
    mp_count = lax.axis_size("mp")
    tokens = acts.shape[0] * dp_count
    strip_rows = BLOCK // dp_count
    owners = jnp.arange(dp_count, dtype=jnp.int32)
    matches = owner_map[:, :, None] == owners[None, None, :]
    where_from = jnp.sum(jnp.where(matches, owners[None, :, None], 0), axis=1)
    blocks_a = acts.reshape(TOK_DEV, NA, BLOCK)
    blocks_g = grads_out.reshape(TOK_DEV, NG, BLOCK)
    sub_rows = strip_rows // mp_count
    row_split = blocks_a.reshape(TOK_DEV, NA, dp_count, mp_count, sub_rows)
    own_rows = lax.dynamic_index_in_dim(row_split, lax.axis_index("mp"), axis=3, keepdims=False)
    a_partial = (
        jnp.einsum("tksr,tkc->ksrc", own_rows, blocks_a, preferred_element_type=jnp.float32)
        / tokens
    )
    g_partial = jnp.einsum("tkb,tkc->kbc", blocks_g, blocks_g, preferred_element_type=jnp.float32)
    g_partial = g_partial.reshape(NG, dp_count, strip_rows, BLOCK)
    a_sent = to_owner(a_partial, where_from[:NA])
    g_sent = to_owner(g_partial, where_from[NA:])
    summed = (
        lax.psum_scatter(a_sent.astype(jnp.bfloat16), "dp", scatter_dimension=1, tiled=True).astype(
            jnp.float32
        ),
        lax.psum_scatter(g_sent.astype(jnp.bfloat16), "dp", scatter_dimension=1, tiled=True).astype(
            jnp.float32
        ),
    )
    a_cov = summed[0]
    a_cov = lax.all_gather(a_cov.astype(jnp.bfloat16), "mp", axis=2, tiled=True).astype(a_cov.dtype)
    g_cov = summed[1]
    a_factor = decay_rate * old_a + (1.0 - decay_rate) * a_cov.reshape(old_a.shape)
    g_factor = decay_rate * old_g + (1.0 - decay_rate) * g_cov.reshape(old_g.shape)
    rows_dev = acts.shape[1] // dp_count
    grad_sum = lax.psum_scatter(
        lax.dot_general(
            acts, grads_out, (((0,), (0,)), ((), ())), preferred_element_type=jnp.float32
        ).astype(jnp.bfloat16),
        "dp",
        scatter_dimension=0,
        tiled=True,
    )
    grad_low = grad_sum.reshape(rows_dev, NG, BLOCK)
    g_blocks = g_inverse.reshape(NG, BLOCK, BLOCK)
    right_done = jnp.einsum("rjb,jbc->rjc", grad_low, g_blocks, preferred_element_type=jnp.float32)
    right_done = right_done.astype(jnp.bfloat16).reshape(rows_dev, FF_DEV)
    column_strip = lax.all_to_all(right_done, "dp", split_axis=1, concat_axis=0, tiled=True)
    inverse_all = lax.all_gather(a_inverse, "dp", axis=0, tiled=True).reshape(NA, BLOCK, BLOCK)
    result = jnp.einsum(
        "kbc,kcf->kbf",
        inverse_all,
        column_strip.reshape(NA, BLOCK, -1),
        preferred_element_type=jnp.float32,
    )
    result = result.astype(jnp.bfloat16).reshape(D_WIN, 1, -1)
    return (a_factor, g_factor, result)


def solution(mesh):
    placed = (
        P("dp", None),
        P("dp", "mp"),
        P("dp", None, None, None),
        P("mp", "dp", None, None, None),
        P("dp", None),
        P("mp", None),
        P(),
    )
    return jax.shard_map(
        per_device,
        mesh=mesh,
        in_specs=placed,
        out_specs=(P("dp", None, None, None), P("mp", "dp", None, None, None), P(None, "mp", "dp")),
        check_vma=False,
    )
```

profile of v0, /device:TPU:0, one launch (start us, length us, event | category | flops | bytes accessed | tf_op | source)
XLA Modules:
  0.0 317.3 jit_solution(11359047946663445373)
XLA Ops:
  7.2 11.7 %convolution_convert_fusion = bf16[3072,2048]{1,0:T(8,128)(2,1)} fusion(bf16[512,3072]{1,0:T(8,128)(2,1)} %param.7, bf16[512,2048]{1,0:T(8,128)(2,1)} %param.8), kind=kOutput, calls=%fused_computation.2 | convolution fusion | flops 6448742400 | bytes 17825792 | tf_op jit(solution)/shard_map/dot_general | solution.py:55
  18.9 0.0 all-reduce.3.cloned.1.call-start
  19.0 0.6 copy-done.1
  19.6 0.1 select_reduce_fusion
  19.7 0.1 reshape.123
  19.8 0.7 copy-done.2
  20.5 4.4 %fusion.1 = bf16[2,1024,1024]{2,1,0:T(8,128)(2,1)} fusion(bf16[64,2,8,1024]{3,2,1,0:T(8,128)(2,1)S(1)} %bitcast.67), kind=kOutput, calls=%fused_computation.6 | convolution fusion | flops 2147483648 | bytes 6291456 | tf_op jit(solution)/shard_map/tkb,tkc->kbc/dot_general | solution.py:36
  24.9 5.0 %gather_fusion.1 = bf16[16,128,1024]{2,1,0:T(8,128)(2,1)} fusion(bf16[2,8,128,1024]{3,2,1,0:T(8,128)(2,1)} %bitcast.62, s32[16]{0:T(128)S(1)} %reshape.123), kind=kCustom, calls=%fused_computation.1 | custom fusion | bytes 8388736 | tf_op jit(solution)/shard_map/jit(take_along_axis)/gather | solution.py:16
  29.8 7.6 %select_convert_fusion = bf16[2,8,128,1024]{3,2,1,0:T(8,128)(2,1)} fusion(bf16[2,8,128,1024]{3,2,1,0:T(8,128)(2,1)} %bitcast.57, pred[2,8]{1,0:T(4,128)(4,1)S(1)} %compare_and_fusion), kind=kLoop, calls=%fused_computation.3 | loop fusion | flops 2097152 | bytes 8388624 | tf_op jit(solution)/shard_map/convert_element_type | solution.py:44
  37.5 0.0 reduce-scatter.6.cloned.1.call-start
  37.5 3.6 %copy.43 = bf16[512,3072]{0,1:T(8,128)(2,1)S(1)} copy(bf16[512,3072]{1,0:T(8,128)(2,1)} %param.7) | data formatting | bytes 6291456 | tf_op args[0]
  41.1 0.1 reshape.117
  41.2 0.1 copy.42
  41.3 2.2 convolution_multiply_fusion
  43.5 2.1 gather_fusion
  45.6 1.7 fusion
  47.3 0.0 all-gather.2.cloned.1.call-start
  47.3 0.5 all-gather.2.cloned.1.call-update
  47.9 66.2 %reduce-scatter.8.cloned.1.call-done = bf16[384,2048]{1,0:T(8,128)(2,1)} async-done(((bf16[3072,2048]{1,0:T(8,128)(2,1)}), bf16[384,2048]{1,0:T(8,128)(2,1)}) %reduce-scatter.8.cloned.1.call-update) | async-done | bytes 1572880 | tf_op jit(solution)/shard_map/reduce_scatter | solution.py:54
  114.1 4.5 %fusion.7 = bf16[384,2,1024]{2,0,1:T(8,128)(2,1)S(1)} fusion(bf16[2,1024,1024]{2,1,0:T(8,128)(2,1)} %bitcast.66, bf16[48,2,8,1024]{3,2,1,0:T(8,128)(2,1)} %bitcast.68), kind=kOutput, calls=%fused_computation.16 | convolution fusion | flops 1611399168 | bytes 7340032 | tf_op jit(solution)/shard_map/rjb,jbc->rjc/dot_general | solution.py:64
  118.5 1.6 copy.50
  120.1 3.8 %all-to-all-start = ((bf16[384,8,256]{0,2,1:T(8,128)(2,1)}), bf16[384,8,256]{0,2,1:T(8,128)(2,1)S(1)}, u32[]{:S(2)}, u32[]{:S(2)}) async-start(bf16[384,8,256]{0,2,1:T(8,128)(2,1)} %bitcast.13), calls=%async_computation.2 | async-start | bytes 3145728 | tf_op jit(solution)/shard_map/all_to_all | solution.py:66
  124.0 0.6 dynamic-slice
  124.5 90.5 %all-reduce.3.cloned.1.call-done = bf16[2,8,128,1024]{3,2,1,0:T(8,128)(2,1)} async-done(((bf16[2,8,128,1024]{3,2,1,0:T(8,128)(2,1)}), bf16[2,8,128,1024]{3,2,1,0:T(8,128)(2,1)}) %all-reduce.3.cloned.1.call-update) | async-done | bytes 4194320
  215.0 3.2 bitcast_add_fusion.1
  218.2 39.1 %reduce-scatter.6.cloned.1.call-done = bf16[3,1,32,1024]{3,2,0,1:T(8,128)(2,1)} async-done(((bf16[3,8,32,1024]{3,2,0,1:T(8,128)(2,1)}), bf16[3,1,32,1024]{3,2,0,1:T(8,128)(2,1)}) %reduce-scatter.6.cloned.1.call-update) | async-done | bytes 196624 | tf_op jit(solution)/shard_map/reduce_scatter | solution.py:41
  257.3 19.9 %all_gather.6 = bf16[3,1,128,1024]{3,2,0,1:T(8,128)(2,1)S(1)} all-gather(bf16[3,1,32,1024]{3,2,0,1:T(8,128)(2,1)} %reduce-scatter.6.cloned.1.call-done), channel_id=1, replica_groups=mesh['dp'=8,'mp'=4] {'mp'}, dimensions={2}, use_global_device_ids=true | all-gather | bytes 983040 | tf_op jit(solution)/shard_map/all_gather | solution.py:49
  277.3 1.4 bitcast_add_fusion
  278.7 0.7 copy.51
  279.5 25.0 %all-gather.2.cloned.1.call-done = bf16[3072,1024]{1,0:T(8,128)(2,1)} async-done(((bf16[384,1024]{1,0:T(8,128)(2,1)}), bf16[3072,1024]{1,0:T(8,128)(2,1)}) %all-gather.2.cloned.1.call-update) | async-done | bytes 6291472 | tf_op jit(solution)/shard_map/all_gather | solution.py:67
  304.5 4.7 %fusion.6 = bf16[3,1024,256]{1,2,0:T(8,128)(2,1)S(1)} fusion(bf16[3,1024,256]{2,1,0:T(8,128)(2,1)S(1)} %bitcast.64, bf16[3,1024,1024]{2,1,0:T(8,128)(2,1)} %bitcast.65), kind=kOutput, calls=%fused_computation.15 | convolution fusion | flops 1611399168 | bytes 9437184 | tf_op jit(solution)/shard_map/kbc,kcf->kbf/dot_general | solution.py:68
  309.2 1.6 copy.53
  (15 shorter events, 0.1 us)
Async XLA Ops:
  7.2 106.9 %reduce-scatter.8.cloned.1.call-start = ((), (), s32[]{:S(2)}) async-start(), calls=%async_computation.4 | async-start | bytes 14155776 | tf_op jit(solution)/shard_map/reduce_scatter | solution.py:54
  18.9 0.7 copy-start.1
  18.9 1.6 copy-start.2
  18.9 196.1 %all-reduce.3.cloned.1.call-start = ((), (), s32[]{:S(2)}) async-start(), calls=%async_computation.6 | async-start | bytes 8388608
  37.5 219.9 %reduce-scatter.6.cloned.1.call-start = ((), (), s32[]{:S(2)}) async-start(), calls=%async_computation.3 | async-start | bytes 1769472 | tf_op jit(solution)/shard_map/reduce_scatter | solution.py:41
  47.3 257.2 %all-gather.2.cloned.1.call-start = ((), (), s32[]{:S(2)}) async-start(), calls=%async_computation.5 | async-start | bytes 7077888 | tf_op jit(solution)/shard_map/all_gather | solution.py:67
  120.1 3.8 %copy-start.3 = (u32[32]{0:T(128)S(1)}, u32[32]{0:T(128)}, u32[]{:S(2)}) copy-start(u32[32]{0:T(128)} %constant.77) | copy-start | bytes 388
  120.1 158.6 %all-to-all-start = ((bf16[384,8,256]{0,2,1:T(8,128)(2,1)}), bf16[384,8,256]{0,2,1:T(8,128)(2,1)S(1)}, u32[]{:S(2)}, u32[]{:S(2)}) async-start(bf16[384,8,256]{0,2,1:T(8,128)(2,1)} %bitcast.13), calls=%async_computation.2 | async-start | bytes 3145728 | tf_op jit(solution)/shard_map/all_to_all | solution.py:66
  123.9 153.3 %copy-start = (f32[1,3,128,1024]{3,2,1,0:T(8,128)S(1)}, f32[1,3,128,1024]{3,2,1,0:T(8,128)}, u32[]{:S(2)}) copy-start(f32[1,3,128,1024]{3,2,1,0:T(8,128)} %param.9) | copy-start | bytes 4718596
Sparse Core Ops, SparseCore 0:
  19.0 94.9 reduce-scatter.7
  117.3 97.6 all-reduce.2
  218.9 38.3 reduce-scatter.5
  259.1 45.3 all-gather.1
where the time goes:
time: 318 us; the launch traced here: 317 us
  waiting for transfers between devices  221 us (69%)
  matrix products  27.4 us (9%)
  blocking collectives  19.9 us (6%)
  local copies, waits for them, and re-layouts  16.7 us (5%)
  other arithmetic  14 us (4%)
  between operations  13.9 us (4%)
  starting transfers between devices  3.97 us (1%)
    unnamed x5, waiting for transfers between devices  91 us
    reduce_scatter x1, waiting for transfers between devices, per_device(): lax.psum_scatter(lax.dot_general(acts, grads_out, (((0,), (0,)), ((), ())...  66.2 us
    reduce_scatter x1, waiting for transfers between devices, per_device(): lax.psum_scatter(a_sent.astype(jnp.bfloat16), 'dp', scatter_dimension=1,...  39.1 us
    all_gather x1, waiting for transfers between devices, per_device(): lax.all_gather(a_inverse, 'dp', axis=0, tiled=True)  25 us
    all_gather x1, blocking collectives, per_device(): lax.all_gather(a_cov.astype(jnp.bfloat16), 'mp', axis=2, tiled=True)  19.9 us
    dot_general x1, matrix products, per_device(): lax.dot_general(acts, grads_out, (((0,), (0,)), ((), ())), preferred_elem...  11.7 us
    convert_element_type x1, other arithmetic, per_device(): g_sent.astype(jnp.bfloat16)  7.62 us
    gather x4, local copies, waits for them, and re-layouts, to_owner(): return jnp.take_along_axis(stacked, where_from[:, :, None, None], axis=1)  7.19 us
  transfers between devices with their start and end apart: 5, of which 4 were waited for; matrix products, arithmetic and copies ran while one was open for 12% of the time, Pallas kernels for 0%

commit v1 on v0

--- a/solution.py
+++ b/solution.py
@@ -46,7 +46,9 @@
         ),
     )
     a_cov = summed[0]
-    a_cov = lax.all_gather(a_cov.astype(jnp.bfloat16), "mp", axis=2, tiled=True).astype(a_cov.dtype)
+    a_cov = jnp.concatenate(lax.all_gather(a_cov.astype(jnp.bfloat16), "mp"), axis=2).astype(
+        a_cov.dtype
+    )
     g_cov = summed[1]
     a_factor = decay_rate * old_a + (1.0 - decay_rate) * a_cov.reshape(old_a.shape)
     g_factor = decay_rate * old_g + (1.0 - decay_rate) * g_cov.reshape(old_g.shape)

time: 318 us -> 294 us (0.925)
  waiting for transfers between devices: 221 us -> 194 us
  matrix products: 27.4 us -> 30.8 us
    reduce_scatter x1 -> x0, waiting for transfers between devices: 39.1 us -> none  [per_device(): lax.psum_scatter(a_sent.astype(jnp.bfloat16), 'dp', scatter_dimension=1,...]
    unnamed x5 -> x4, waiting for transfers between devices: 91 us -> 109 us
    all_gather x1, waiting for transfers between devices: 25 us -> 19.6 us  [per_device(): lax.all_gather(a_inverse, 'dp', axis=0, tiled=True)]
    dot_general x1, matrix products: 4.36 us -> 7.83 us  [per_device(): jnp.einsum('tkb,tkc->kbc', blocks_g, blocks_g, preferred_element_type=jnp...]
    unnamed x10 -> x11, local copies, waits for them, and re-layouts: 5.52 us -> 6.42 us
  transfers between devices with their start and end apart: 5 -> 4, of which waited for: 4 -> 3; matrix products, arithmetic and copies ran while one was open for 12% -> 15% of each run, Pallas kernels for 0% -> 0%
where the time goes in v1:
time: 294 us; the launch traced here: 293 us
  waiting for transfers between devices  194 us (66%)
  matrix products  30.8 us (10%)
  blocking collectives  19.7 us (7%)
  local copies, waits for them, and re-layouts  18.8 us (6%)
  between operations  13.9 us (5%)
  other arithmetic  12 us (4%)
  starting transfers between devices  3.83 us (1%)
    unnamed x4, waiting for transfers between devices  109 us
    reduce_scatter x1, waiting for transfers between devices, per_device(): lax.psum_scatter(lax.dot_general(acts, grads_out, (((0,), (0,)), ((), ())...  65.2 us
    all_gather x1, blocking collectives, per_device(): lax.all_gather(a_cov.astype(jnp.bfloat16), 'mp')  19.7 us
    all_gather x1, waiting for transfers between devices, per_device(): lax.all_gather(a_inverse, 'dp', axis=0, tiled=True)  19.6 us
    dot_general x1, matrix products, per_device(): lax.dot_general(acts, grads_out, (((0,), (0,)), ((), ())), preferred_elem...  11.7 us
    gather x4, local copies, waits for them, and re-layouts, to_owner(): return jnp.take_along_axis(stacked, where_from[:, :, None, None], axis=1)  8.35 us
    dot_general x1, matrix products, per_device(): jnp.einsum('tkb,tkc->kbc', blocks_g, blocks_g, preferred_element_type=jnp...  7.83 us
    unnamed x11, local copies, waits for them, and re-layouts  6.42 us
  transfers between devices with their start and end apart: 4, of which 3 were waited for; matrix products, arithmetic and copies ran while one was open for 15% of the time, Pallas kernels for 0%

profile of v1, /device:TPU:0, one launch (start us, length us, event | category | flops | bytes accessed | tf_op | source)
XLA Modules:
  0.0 293.3 jit_solution(820730358544375701)
XLA Ops:
  7.2 0.0 reduce-scatter.8.cloned.1.call-start
  7.2 11.7 %convolution_convert_fusion = bf16[3072,2048]{1,0:T(8,128)(2,1)} fusion(bf16[512,3072]{1,0:T(8,128)(2,1)} %param.7, bf16[512,2048]{1,0:T(8,128)(2,1)} %param.8), kind=kOutput, calls=%fused_computation.2 | convolution fusion | flops 6448742400 | bytes 17825792 | tf_op jit(solution)/shard_map/dot_general | solution.py:57
  18.9 0.0 all-reduce.5.cloned.1.call-start
  19.0 3.2 %copy.39 = bf16[512,3072]{0,1:T(8,128)(2,1)S(1)} copy(bf16[512,3072]{1,0:T(8,128)(2,1)} %param.7) | data formatting | bytes 6291456 | tf_op args[0]
  22.2 0.1 select_reduce_fusion
  22.3 0.1 reshape.127
  22.4 0.1 reshape.133
  22.5 2.2 convolution_multiply_fusion
  24.6 2.1 gather_fusion
  26.7 7.8 %fusion = bf16[2,1024,1024]{2,1,0:T(8,128)(2,1)} fusion(bf16[64,2,8,1024]{3,2,1,0:T(8,128)(2,1)} %bitcast.77), kind=kOutput, calls=%fused_computation.5 | convolution fusion | flops 2147483648 | bytes 6291456 | tf_op jit(solution)/shard_map/tkb,tkc->kbc/dot_general | solution.py:36
  34.5 6.1 %gather_fusion.1 = bf16[16,128,1024]{2,1,0:T(8,128)(2,1)} fusion(bf16[2,8,128,1024]{3,2,1,0:T(8,128)(2,1)} %bitcast.72, s32[16]{0:T(128)S(1)} %reshape.133), kind=kCustom, calls=%fused_computation.1 | custom fusion | bytes 8388736 | tf_op jit(solution)/shard_map/jit(take_along_axis)/gather | solution.py:16
  40.7 1.7 select_convert_fusion.1
  42.4 5.8 %select_convert_fusion = bf16[2,8,128,1024]{3,2,1,0:T(8,128)(2,1)} fusion(bf16[2,8,128,1024]{3,2,1,0:T(8,128)(2,1)} %bitcast.66, pred[2,8]{1,0:T(4,128)(4,1)S(1)} %compare_and_fusion), kind=kLoop, calls=%fused_computation.3 | loop fusion | flops 2097152 | bytes 8388624 | tf_op jit(solution)/shard_map/convert_element_type | solution.py:44
  48.2 0.0 all-gather.3.cloned.1.call-start
  48.2 0.7 all-gather.3.cloned.1.call-update
  48.9 65.2 %reduce-scatter.8.cloned.1.call-done = bf16[384,2048]{1,0:T(8,128)(2,1)} async-done(((bf16[3072,2048]{1,0:T(8,128)(2,1)}), bf16[384,2048]{1,0:T(8,128)(2,1)}) %reduce-scatter.8.cloned.1.call-update) | async-done | bytes 1572880 | tf_op jit(solution)/shard_map/reduce_scatter | solution.py:56
  114.1 4.5 %fusion.6 = bf16[384,2,1024]{2,0,1:T(8,128)(2,1)S(1)} fusion(bf16[2,1024,1024]{2,1,0:T(8,128)(2,1)} %bitcast.76, bf16[48,2,8,1024]{3,2,1,0:T(8,128)(2,1)} %bitcast.78), kind=kOutput, calls=%fused_computation.16 | convolution fusion | flops 1611399168 | bytes 7340032 | tf_op jit(solution)/shard_map/rjb,jbc->rjc/dot_general | solution.py:66
  118.5 1.6 copy.46
  120.1 3.7 %all-to-all-start = ((bf16[384,8,256]{0,2,1:T(8,128)(2,1)}), bf16[384,8,256]{0,2,1:T(8,128)(2,1)S(1)}, u32[]{:S(2)}, u32[]{:S(2)}) async-start(bf16[384,8,256]{0,2,1:T(8,128)(2,1)} %bitcast.15), calls=%async_computation.1 | async-start | bytes 3145728 | tf_op jit(solution)/shard_map/all_to_all | solution.py:68
  123.8 0.6 dynamic-slice
  124.4 108.7 %all-reduce.5.cloned.1.call-done = (bf16[3,8,32,1024]{3,2,1,0:T(8,128)(2,1)}, bf16[2,8,128,1024]{3,2,1,0:T(8,128)(2,1)}) async-done(((bf16[3,8,32,1024]{3,2,1,0:T(8,128)(2,1)}, bf16[2,8,128,1024]{3,2,1,0:T(8,128)(2,1)}), (bf16[3,8,32,1024]{3,2,1,0:T(8,128)(2,1)}, bf16[2,8,128,1024]{3,2,1,0:T(8,128)(2,1)})) %all-reduce.5.cloned.1.call-update) | async-done | bytes 5767184
  233.1 1.6 constant_dynamic-slice_fusion
  234.7 19.7 %all-gather = bf16[12,1,32,1024]{3,2,1,0:T(8,128)(2,1)S(1)} all-gather(bf16[3,1,32,1024]{3,2,1,0:T(8,128)(2,1)S(1)} %constant_dynamic-slice_fusion), channel_id=2, replica_groups=mesh['dp'=8,'mp'=4] {'mp'}, dimensions={0}, use_global_device_ids=true | all-gather | bytes 983040 | tf_op jit(solution)/shard_map/all_gather | solution.py:49
  254.4 0.2 convert_multiply_fusion
  254.6 0.2 copy.42
  254.8 1.0 copy-done.1
  255.8 2.8 bitcast_add_fusion.1
  258.6 1.4 bitcast_add_fusion
  260.1 0.7 copy.47
  260.8 19.6 %all-gather.3.cloned.1.call-done = bf16[3072,1024]{1,0:T(8,128)(2,1)} async-done(((bf16[384,1024]{1,0:T(8,128)(2,1)}), bf16[3072,1024]{1,0:T(8,128)(2,1)}) %all-gather.3.cloned.1.call-update) | async-done | bytes 6291472 | tf_op jit(solution)/shard_map/all_gather | solution.py:69
  280.5 4.7 %fusion.5 = bf16[3,1024,256]{1,2,0:T(8,128)(2,1)S(1)} fusion(bf16[3,1024,256]{2,1,0:T(8,128)(2,1)S(1)} %bitcast.74, bf16[3,1024,1024]{2,1,0:T(8,128)(2,1)} %bitcast.75), kind=kOutput, calls=%fused_computation.15 | convolution fusion | flops 1611399168 | bytes 9437184 | tf_op jit(solution)/shard_map/kbc,kcf->kbf/dot_general | solution.py:70
  285.2 1.6 copy.49
  (14 shorter events, 0.1 us)
Async XLA Ops:
  7.2 106.9 %reduce-scatter.8.cloned.1.call-start = ((), (), s32[]{:S(2)}) async-start(), calls=%async_computation.2 | async-start | bytes 14155776 | tf_op jit(solution)/shard_map/reduce_scatter | solution.py:56
  18.9 214.2 %all-reduce.5.cloned.1.call-start = ((), (), s32[]{:S(2)}) async-start(), calls=%async_computation.4 | async-start | bytes 11534336
  19.0 3.2 %copy-start.2 = (s32[5,8]{1,0:T(8,128)S(1)}, s32[5,8]{1,0:T(8,128)}, u32[]{:S(2)}) copy-start(s32[5,8]{1,0:T(8,128)} %param.13) | copy-start | bytes 484
  48.2 232.3 %all-gather.3.cloned.1.call-start = ((), (), s32[]{:S(2)}) async-start(), calls=%async_computation.3 | async-start | bytes 7077888 | tf_op jit(solution)/shard_map/all_gather | solution.py:69
  120.1 3.7 %copy-start.3 = (u32[32]{0:T(128)S(1)}, u32[32]{0:T(128)}, u32[]{:S(2)}) copy-start(u32[32]{0:T(128)} %constant.77) | copy-start | bytes 388
  120.1 140.0 %all-to-all-start = ((bf16[384,8,256]{0,2,1:T(8,128)(2,1)}), bf16[384,8,256]{0,2,1:T(8,128)(2,1)S(1)}, u32[]{:S(2)}, u32[]{:S(2)}) async-start(bf16[384,8,256]{0,2,1:T(8,128)(2,1)} %bitcast.15), calls=%async_computation.1 | async-start | bytes 3145728 | tf_op jit(solution)/shard_map/all_to_all | solution.py:68
  254.6 1.2 copy-start.1
  254.8 3.9 %copy-start = (f32[1,3,128,1024]{3,2,1,0:T(8,128)S(1)}, f32[1,3,128,1024]{3,2,1,0:T(8,128)}, u32[]{:S(2)}) copy-start(f32[1,3,128,1024]{3,2,1,0:T(8,128)} %param.9) | copy-start | bytes 4718596
Sparse Core Ops, SparseCore 0:
  19.0 94.9 reduce-scatter.7
  118.0 114.9 all-reduce.4
  235.0 45.4 all-gather.2
